TPU v7x, 256 devices: a whole 4x4x8 slice. The times are simulated.
256 devices in a mesh: row: 32 (over y, z), col: 8 (over x, core).
Axes of the slice: x: 4, y: 4, z: 8, core: 2. Of those that a mesh axis runs over, the one named last changes fastest.
Arguments:
- features: bfloat16 [49152, 4096], P(('row', 'col')), may hold values from -24 to 24
- cotangent: bfloat16 [49152, 8192], P(('row', 'col')), may hold values from -0.02734375 to 0.02734375
Outputs:
- weight_grad: float32 [4096, 8192], P('row', 'col')
All inputs are finite; a program needn't handle non-finite values.
Results may differ from a plain program's by a relative error of at most 0.0003.
Values may be sent and summed in bfloat16 or wider, within the bound.
A program may use at most 256 MiB of HBM per device.

v0:
```python
import jax
import jax.numpy as jnp
from jax import lax
from jax.sharding import Mesh
from jax.sharding import PartitionSpec as P

ROW = ("row_0", "row_1")
ROW_COL = ("row_0", "row_1", "col")


def sum_by_axis(array, axes, dim):
    for axis in axes:
        array = lax.psum_scatter(array, axis, scatter_dimension=dim, tiled=True)
    return array


def tokens_product(left, right):
    return lax.dot_general(
        left, right, (((0,), (0,)), ((), ())), preferred_element_type=jnp.float32
    )


def local(features, cotangent):
    columns = lax.all_to_all(cotangent, "col", split_axis=1, concat_axis=0, tiled=True)
    partial_value = tokens_product(lax.all_gather(features, "col", axis=0, tiled=True), columns)
    return sum_by_axis(partial_value, ROW, 0)


def solution(mesh):
    torus = Mesh(mesh.devices.reshape(4, 8, mesh.shape["col"]), ("row_0", "row_1", "col"))
    in_specs = (P(ROW_COL, None), P(ROW_COL, None))
    out_specs = P(ROW, "col")
    return jax.shard_map(local, mesh=torus, in_specs=in_specs, out_specs=out_specs, check_vma=False)
```

profile of v0, /device:TPU:1, one launch (start us, length us, event | category | flops | bytes accessed | tf_op | source)
XLA Modules:
  0.0 340.8 jit_solution(15472205882023542649)
XLA Ops:
  6.5 0.0 all-gather.2.cloned.1.call-start
  6.5 0.7 all-gather.2.cloned.1.call-update
  7.3 0.0 reduce-scatter.3.cloned.1.call-start
  7.3 2.3 copy.7
  9.6 65.5 %all_to_all.19 = bf16[192,8,1024]{2,0,1:T(8,128)(2,1)S(1)} all-to-all(bf16[192,8,1024]{2,0,1:T(8,128)(2,1)S(1)} %bitcast.9), channel_id=1, replica_groups=mesh['row_0'=4,'row_1'=8,'col'=8] {'col'}, dimensions={1} | all-to-all | bytes 6291456 | tf_op jit(solution)/shard_map/all_to_all | solution.py:24
  75.1 30.6 %all-gather.2.cloned.1.call-done = bf16[1536,4096]{1,0:T(8,128)(2,1)} async-done(((bf16[192,4096]{1,0:T(8,128)(2,1)}), bf16[1536,4096]{1,0:T(8,128)(2,1)}) %all-gather.2.cloned.1.call-update) | async-done | bytes 12582928 | tf_op jit(solution)/shard_map/all_gather | solution.py:25
  105.7 19.5 %fusion = f32[4096,1024]{1,0:T(8,128)} fusion(bf16[1536,4096]{1,0:T(8,128)(2,1)} %all-gather.2.cloned.1.call-done, bf16[1536,1024]{1,0:T(8,128)(2,1)S(1)} %bitcast.11), kind=kOutput, calls=%fused_computation.1 | convolution fusion | flops 12884901888 | bytes 32505856 | tf_op jit(solution)/shard_map/dot_general | solution.py:18
  125.2 0.0 reduce-scatter.3.cloned.1.call-update
  125.3 0.0 reduce-scatter.5.cloned.1.call-start
  125.3 151.3 %reduce-scatter.3.cloned.1.call-done = f32[1024,1024]{1,0:T(8,128)} async-done(((f32[4096,1024]{1,0:T(8,128)}), f32[1024,1024]{1,0:T(8,128)}) %reduce-scatter.3.cloned.1.call-update) | async-done | bytes 4194320 | tf_op jit(solution)/shard_map/reduce_scatter | solution.py:13
  276.6 0.0 reduce-scatter.5.cloned.1.call-update
  276.6 57.6 %reduce-scatter.5.cloned.1.call-done = f32[128,1024]{1,0:T(8,128)} async-done(((f32[1024,1024]{1,0:T(8,128)}), f32[128,1024]{1,0:T(8,128)}) %reduce-scatter.5.cloned.1.call-update) | async-done | bytes 524304 | tf_op jit(solution)/shard_map/reduce_scatter | solution.py:13
Async XLA Ops:
  6.5 99.2 %all-gather.2.cloned.1.call-start = ((), (), s32[]{:S(2)}) async-start(), calls=%async_computation.3 | async-start | bytes 14155776 | tf_op jit(solution)/shard_map/all_gather | solution.py:25
  7.3 269.4 %reduce-scatter.3.cloned.1.call-start = ((), (), s32[]{:S(2)}) async-start(), calls=%async_computation.4 | async-start | bytes 20971520 | tf_op jit(solution)/shard_map/reduce_scatter | solution.py:13
  125.3 209.0 %reduce-scatter.5.cloned.1.call-start = ((), (), s32[]{:S(2)}) async-start(), calls=%async_computation.5 | async-start | bytes 4718592 | tf_op jit(solution)/shard_map/reduce_scatter | solution.py:13
Sparse Core Ops, SparseCore 0:
  9.2 96.4 all-gather.1
  125.4 151.1 reduce-scatter.2
  279.2 55.0 reduce-scatter.4
where the time goes:
time: 341 us
  waiting for transfers between devices  240 us (70%)
  blocking collectives  65.5 us (19%)
  matrix products  19.5 us (6%)
  between operations  13.1 us (4%)
    reduce_scatter x2, waiting for transfers between devices, sum_by_axis(): array = lax.psum_scatter(array, axis, scatter_dimension=dim, tiled=True)  209 us
    all_to_all x1, blocking collectives, local(): lax.all_to_all(cotangent, 'col', split_axis=1, concat_axis=0, tiled=True)  65.5 us
    all_gather x1, waiting for transfers between devices, local(): lax.all_gather(features, 'col', axis=0, tiled=True)  30.6 us
    dot_general x1, matrix products, tokens_product(): lax.dot_general(left, right, (((0,), (0,)), ((), ())), preferred_element_...  19.5 us
  transfers between devices with their start and end apart: 3, of which 3 were waited for; matrix products, arithmetic and copies ran while one was open for 1% of the time, Pallas kernels for 0%

commit v1 on v0

v1 whole, which is shorter than its diff:
```python
import jax
import jax.numpy as jnp
from jax import lax
from jax.experimental import pallas as pl
from jax.experimental.pallas import tpu as pltpu
from jax.sharding import PartitionSpec as P

NX, NY, NZ = 4, 4, 8
TOK = 192
HALF = TOK // 2
GROUP = 8 * TOK
COLS = 1024
BLK = 128
CHUNK = NY * BLK
N = NZ
TILE = 128
H = COLS // 2

POWER = 32
LOW = 2.0**-3.9
SPAN = 2.0**3.9 - 2.0**-3.9
PAD = 16

f32, bf16 = jnp.float32, jnp.bfloat16


def rows(start, size):
    return pl.ds(pl.multiple_of(start, 32), size)


def tile(t):
    return pl.ds(pl.multiple_of(t * TILE, TILE), TILE)


def encode(read, first, tiles, message):
    def widest(t, most):
        value = jnp.abs(read(first + t))
        return jnp.maximum(most, jnp.max(value.reshape(TILE // 8, 8, BLK), axis=0))

    most = lax.fori_loop(0, tiles, widest, jnp.zeros((8, BLK), f32))
    most = jnp.maximum(jnp.max(most, axis=0, keepdims=True) * 1.01, 1e-30)
    most = jnp.broadcast_to(most, (PAD, BLK)).astype(bf16)
    message[pl.ds(tiles * TILE, PAD), :] = most
    scale = SPAN / most.astype(f32)[:1]

    def code(t, _):
        value = read(first + t)
        power = jnp.abs(value) * scale + LOW
        for _ in range(5):
            power = power * power
        message[tile(t), :] = jnp.where(value < 0, -power, power).astype(bf16)
        return 0

    lax.fori_loop(0, tiles, code, 0)


def decoder(message, tiles):
    scale = message[pl.ds(tiles * TILE, PAD), :].astype(f32)[:1] * (1.0 / SPAN)

    def decode(t):
        value = message[tile(t), :].astype(f32)
        root = jnp.exp2(jnp.log(jnp.abs(value)) * (1.4426950408889634 / POWER))
        size = (root - LOW) * scale
        return jnp.where(value < 0, -size, size)

    return decode


def kernel(
    f_in, c_in, out, f_all, c_all, relay, ct, pt, s1, r1, s2, r2, zs, zr,
    f_own, c_own, c_out, c_far_out, c_get, c_far, c_relay,
    f_out, f_pass, f_relay, f_get, y1_out, y1_get, y2_out, y2_get, z_out, z_get,
):
    row, col = lax.axis_index("row"), lax.axis_index("col")
    y, z = lax.div(row, NZ), lax.rem(row, NZ)
    x, k = lax.div(col, 2), lax.rem(col, 2)

    def on_x(step, core):
        return {"row": row, "col": lax.rem(x + step + NX, NX) * 2 + core}

    def on_y(step):
        return {"row": lax.rem(y + step + NY, NY) * NZ + z, "col": col}

    def on_z(step):
        return {"row": y * NZ + lax.rem(z + step + NZ, NZ), "col": col}

    def place(step, core):
        return lax.rem(x + step + NX, NX) * 2 + core

    def send(src, dst, out_sem, get_sem, to):
        return pltpu.make_async_remote_copy(
            src_ref=src, dst_ref=dst, send_sem=out_sem, recv_sem=get_sem,
            device_id=to, device_id_type=pl.DeviceIdType.MESH,
        )

    partner = on_x(0, 1 - k)

    def offset(n):
        far = N // 2 - lax.div(n + 1, 2)
        return lax.rem(z + far * (2 * lax.rem(n, 2) - 1) + NZ, NZ)

    def own_features(n, _):
        for yy in range(NY):
            at = pl.multiple_of((yy * NZ + offset(n)) * BLK, BLK)
            pltpu.make_async_copy(
                f_in.at[:, pl.ds(at, BLK)],
                f_all.at[n, rows(col * TOK, TOK), pl.ds(yy * BLK, BLK)],
                f_own.at[n],
            ).start()
        return 0

    def columns(device):
        return pl.ds(pl.multiple_of(device * COLS, COLS), COLS)

    lax.fori_loop(0, N, own_features, 0)
    keep = pltpu.make_async_copy(
        c_in.at[:, columns(col)], c_all.at[rows(col * TOK, TOK), :], c_own.at[0]
    )
    keep.start()

    barrier = pltpu.get_barrier_semaphore()
    peers = [partner] + [on_x(d, c) for d in (1, -1) for c in (0, 1)]
    peers += [on_y(1), on_y(-1), on_z(1), on_z(-1)]
    for peer in peers:
        pl.semaphore_signal(
            barrier, inc=1, device_id=peer, device_id_type=pl.DeviceIdType.MESH
        )
    pl.semaphore_wait(barrier, len(peers))

    ways = ((0, 1), (1, -1))

    def far_first(way, d, c):
        return send(
            c_in.at[pl.ds(way * HALF, HALF), columns(place(2, c))],
            relay.at[way * 2 + c], c_far_out.at[way * 2 + c], c_relay.at[way * 2 + c],
            on_x(d, k),
        )

    def far_second(way, d, c):
        at = rows(place(-d, k) * TOK + way * HALF, HALF)
        return send(
            relay.at[way * 2 + c], c_all.at[at, :],
            c_far_out.at[4 + way * 2 + c], c_far.at[way * 2 + k], on_x(d, c),
        )

    def near(step, c, slot):
        return send(
            c_in.at[:, columns(place(step, c))], c_all.at[rows(col * TOK, TOK), :],
            c_out.at[slot], c_get.at[col], on_x(step, c),
        )

    nears = [near(d, c, way * 2 + c) for way, d in ways for c in (0, 1)]
    nears.append(near(0, 1 - k, 4))
    for way, d in ways:
        for c in (0, 1):
            far_first(way, d, c).start()
    for copy in nears:
        copy.start()

    def block(n, device):
        return f_all.at[n, rows(device * TOK, TOK), :]

    def pass_on(n, device, out_sem, to):
        return send(block(n, device), block(n, device), out_sem, f_get.at[n, device], to)

    def own_out(n):
        return [
            pass_on(n, col, f_out.at[n, 0], on_x(1, k)),
            pass_on(n, col, f_out.at[n, 1], on_x(-1, k)),
            pass_on(n, col, f_out.at[n, 2], partner),
        ]

    def to_partner(n, step, slot):
        return pass_on(n, place(step, k), f_pass.at[n, slot], partner)

    def relayed(n):
        d = 1 - 2 * lax.rem(n, 2)
        return pass_on(n, place(-d, k), f_relay.at[n], on_x(d, k))

    def arrived(n, device):
        pass_on(n, device, f_out.at[n, 0], f_partner).wait_recv()

    f_partner = partner

    def x0(n):
        pltpu.make_async_copy(
            f_in.at[:, pl.ds(0, CHUNK)], block(n, col), f_own.at[n]
        ).wait()
        for copy in own_out(n):
            copy.start()

    def x1(n):
        arrived(n, place(1, k))
        arrived(n, place(-1, k))
        relayed(n).start()
        to_partner(n, 1, 0).start()
        to_partner(n, -1, 1).start()

    def x2(n):
        arrived(n, place(2, k))
        to_partner(n, 2, 2).start()

    x0(0)
    for way, d in ways:
        for c in (0, 1):
            far_first(way, d, c).wait_recv()
            far_second(way, d, c).start()
    x0(1)
    x0(2)
    x1(0)
    x2(0)

    keep.wait()
    for step, c in ((0, 1 - k), (1, 0), (1, 1), (-1, 0), (-1, 1)):
        send(
            c_in.at[:, columns(0)], c_all.at[rows(0, TOK), :],
            c_out.at[0], c_get.at[place(step, c)], partner,
        ).wait_recv()
    for i in range(4):
        send(
            relay.at[i], c_all.at[rows(0, HALF), :], c_out.at[0], c_far.at[i], partner
        ).wait_recv()

    def transpose(t, _):
        ct[:, tile(t)] = c_all[tile(t), :].T
        return 0

    lax.fori_loop(0, GROUP // TILE, transpose, 0)

    y_up, y_down = lax.rem(y + 1, NY), lax.rem(y + 3, NY)
    y_far = lax.rem(y + 2, NY)

    def first_out(n):
        return [
            send(s1.at[n, i], r1.at[n, i], y1_out.at[n, i], y1_get.at[n, i], on_y(d))
            for i, d in ways
        ]

    def second_out(n):
        return [
            send(s2.at[n, i], r2.at[n, i], y2_out.at[n, i], y2_get.at[n, i], on_y(d))
            for i, d in ways
        ]

    def a(n):
        slot = lax.rem(n, 4)
        for c in range(NX):
            arrived(n, c * 2 + 1 - k)

        def product(m, _):
            at = pl.ds(pl.multiple_of(m * 256, 256), 256)
            value = jnp.dot(ct[at, :], f_all[n], preferred_element_type=f32)
            for yy in range(NY):
                pt[slot, yy, at, :] = value[:, yy * BLK : (yy + 1) * BLK]
            return 0

        lax.fori_loop(0, COLS // 256, product, 0)
        half = H // TILE
        for i in (0, 1):
            encode(lambda t: pt[slot, y_far, tile(t), :], i * half, half, s1.at[n, i])
        for copy in first_out(n):
            copy.start()

    def b(n):
        slot = lax.rem(n, 4)
        half = H // TILE
        arriving = first_out(n)
        leaving = second_out(n)
        for i, target in ((0, y_up), (1, y_down)):
            arriving[i].wait_recv()
            decode = decoder(r1.at[n, i], half)

            def add(t, _):
                at = tile(i * half + t)
                pt[slot, target, at, :] += decode(t)
                return 0

            lax.fori_loop(0, half, add, 0)
            encode(lambda t: pt[slot, target, tile(t), :], 0, COLS // TILE, s2.at[n, i])
            leaving[i].start()

    whole = COLS + PAD
    part = H + PAD

    def z_half(i, d):
        return send(
            zs.at[i * 7, pl.ds(0, part), :], zr.at[i * 7, pl.ds(0, part), :],
            z_out.at[i * 7], z_get.at[i * 7], on_z(d),
        )

    def z_whole(n):
        d = 2 * lax.rem(n, 2) - 1
        return send(zs.at[n], zr.at[n], z_out.at[n], z_get.at[n], on_z(d))

    def c(n):
        slot = lax.rem(n, 4)
        half = H // TILE
        arriving = second_out(n)
        arriving[0].wait_recv()
        arriving[1].wait_recv()
        up = decoder(r2.at[n, 0], COLS // TILE)
        down = decoder(r2.at[n, 1], COLS // TILE)

        def total(t, _):
            pt[slot, y, tile(t), :] += up(t) + down(t)
            return 0

        lax.fori_loop(0, COLS // TILE, total, 0)

        def read(t):
            return pt[slot, y, tile(t), :]

        def join(message, tiles, first):
            decode = decoder(message, tiles)

            def add(t, _):
                pt[slot, y, tile(first + t), :] += decode(t)
                return 0

            lax.fori_loop(0, tiles, add, 0)

        @pl.when(n == 0)
        def _():
            for i, d in ways:
                encode(read, i * half, half, zs.at[i * 7])
                z_half(i, d).start()

        @pl.when(n == 1)
        def _():
            z_half(0, 1).wait_recv()
            join(zr.at[0], half, 0)

        @pl.when(n == 2)
        def _():
            z_half(1, -1).wait_recv()
            join(zr.at[7], half, half)

        @pl.when(n >= 3)
        def _():
            z_whole(n - 2).wait_recv()
            join(zr.at[n - 2], COLS // TILE, 0)

        @pl.when((n >= 1) & (n < N - 1))
        def _():
            encode(read, 0, COLS // TILE, zs.at[n])
            z_whole(n).start()

        @pl.when(n == N - 1)
        def _():
            z_whole(n - 1).wait_recv()
            join(zr.at[n - 1], COLS // TILE, 0)

            def put(t, _):
                out[:, tile(t)] = pt[slot, y, tile(t), :].T
                return 0

            lax.fori_loop(0, COLS // TILE, put, 0)

    def step(it, _):
        @pl.when(it < N)
        def _():
            a(it)

        @pl.when(it == 0)
        def _():
            x1(1)

        @pl.when(it < N - 3)
        def _():
            x0(it + 3)

        @pl.when(it < N - 2)
        def _():
            x1(it + 2)

        @pl.when((it >= 1) & (it < N + 1))
        def _():
            b(it - 1)

        @pl.when(it < N - 1)
        def _():
            x2(it + 1)

        @pl.when(it >= 2)
        def _():
            c(it - 2)

        return 0

    lax.fori_loop(0, N + 2, step, 0)

    for way, d in ways:
        for core in (0, 1):
            far_first(way, d, core).wait_send()
            far_second(way, d, core).wait_send()
        z_half(way, d).wait_send()
    for copy in nears:
        copy.wait_send()

    def drain(n, _):
        for copy in own_out(n) + first_out(n) + second_out(n):
            copy.wait_send()
        for i, hop in enumerate((1, -1, 2)):
            to_partner(n, hop, i).wait_send()
        relayed(n).wait_send()
        return 0

    lax.fori_loop(0, N, drain, 0)

    def drain_z(n, _):
        z_whole(n).wait_send()
        return 0

    lax.fori_loop(1, N - 1, drain_z, 0)


def local(features, cotangent):
    dma = pltpu.SemaphoreType.DMA
    return pl.pallas_call(
        kernel,
        out_shape=jax.ShapeDtypeStruct((BLK, COLS), f32),
        in_specs=[pl.BlockSpec(memory_space=pl.ANY)] * 2,
        out_specs=pl.BlockSpec(memory_space=pltpu.VMEM),
        scratch_shapes=[
            pltpu.VMEM((N, GROUP, CHUNK), bf16),
            pltpu.VMEM((GROUP, COLS), bf16),
            pltpu.VMEM((4, HALF, COLS), bf16),
            pltpu.VMEM((COLS, GROUP), bf16),
            pltpu.VMEM((4, NY, COLS, BLK), f32),
            pltpu.VMEM((N, 2, H + PAD, BLK), bf16),
            pltpu.VMEM((N, 2, H + PAD, BLK), bf16),
            pltpu.VMEM((N, 2, COLS + PAD, BLK), bf16),
            pltpu.VMEM((N, 2, COLS + PAD, BLK), bf16),
            pltpu.VMEM((N, COLS + PAD, BLK), bf16),
            pltpu.VMEM((N, COLS + PAD, BLK), bf16),
            dma((N,)), dma((1,)), dma((5,)), dma((8,)), dma((8,)), dma((4,)), dma((4,)),
            dma((N, 3)), dma((N, 3)), dma((N,)), dma((N, 8)),
            dma((N, 2)), dma((N, 2)), dma((N, 2)), dma((N, 2)), dma((N,)), dma((N,)),
        ],
        compiler_params=pltpu.CompilerParams(
            collective_id=0, has_side_effects=True, vmem_limit_bytes=62 * 1024 * 1024
        ),
        name="weight_grad",
    )(features, cotangent)


def solution(mesh):
    return jax.shard_map(
        local,
        mesh=mesh,
        in_specs=(P(("row", "col"), None), P(("row", "col"), None)),
        out_specs=P("row", "col"),
        check_vma=False,
    )
```

time: 341 us -> 151 us (0.44)
  waiting for transfers between devices: 240 us -> 0 us
  Pallas kernels: 0 us -> 149 us
  blocking collectives: 65.5 us -> 0 us
  matrix products: 19.5 us -> 0 us
  between operations: 13.1 us -> 0.01 us
    reduce_scatter x2 -> x0, waiting for transfers between devices: 209 us -> none  [sum_by_axis(): array = lax.psum_scatter(array, axis, scatter_dimension=dim, tiled=True)]
    pallas_call x0 -> x1, Pallas kernels: none -> 149 us  [local(): pl.pallas_call(kernel, out_shape=jax.ShapeDtypeStruct((BLK, COLS), f32),...]
    all_to_all x1 -> x0, blocking collectives: 65.5 us -> none  [local(): lax.all_to_all(cotangent, 'col', split_axis=1, concat_axis=0, tiled=True)]
    all_gather x1 -> x0, waiting for transfers between devices: 30.6 us -> none  [local(): lax.all_gather(features, 'col', axis=0, tiled=True)]
    dot_general x1 -> x0, matrix products: 19.5 us -> none  [tokens_product(): lax.dot_general(left, right, (((0,), (0,)), ((), ())), preferred_element_...]
  transfers between devices with their start and end apart: 3 -> 0, of which waited for: 3 -> 0; matrix products, arithmetic and copies ran while one was open for 1% -> 0% of each run, Pallas kernels for 0% -> 0%
where the time goes in v1:
time: 151 us
  Pallas kernels  149 us (99%)
  local copies, waits for them, and re-layouts  1.89 us (1%)
    pallas_call x1, Pallas kernels, local(): pl.pallas_call(kernel, out_shape=jax.ShapeDtypeStruct((BLK, COLS), f32),...  149 us

profile of v1, /device:TPU:1, one launch (start us, length us, event | category | flops | bytes accessed | tf_op | source)
XLA Modules:
  0.0 150.6 jit_solution(2612530704572841976)
XLA Ops:
  0.0 148.7 %weight_grad.1 = f32[128,1024]{1,0:T(8,128)} custom-call(bf16[192,4096]{1,0:T(8,128)(2,1)} %f_in.1, bf16[192,8192]{1,0:T(8,128)(2,1)} %c_in.1), custom_call_target="tpu_custom_call" | custom-call | tf_op jit(solution)/shard_map/weight_grad/pallas_call | solution.py:419
  148.7 1.9 %copy.4 = f32[128,1024]{1,0:T(8,128)} copy(f32[128,1024]{1,0:T(8,128)} %weight_grad.1) | data formatting | bytes 1048576

commit v2 on v1

--- a/solution.py
+++ b/solution.py
@@ -13,8 +13,12 @@
 BLK = 128
 CHUNK = NY * BLK
 N = NZ
-TILE = 128
-H = COLS // 2
+TILE = 32
+WIDE = 128
+LATE = 320
+EARLY = COLS - LATE
+H = EARLY // 2
+L = LATE // 2
 
 POWER = 32
 LOW = 2.0**-3.9
@@ -32,26 +36,50 @@
     return pl.ds(pl.multiple_of(t * TILE, TILE), TILE)
 
 
+def wide(t):
+    return pl.ds(pl.multiple_of(t * WIDE, WIDE), WIDE)
+
+
+def each(count, body):
+    step = next(u for u in range(12, 0, -1) if count % u == 0)
+
+    def group(g, _):
+        for i in range(step):
+            body(g * step + i)
+        return 0
+
+    if count == step:
+        group(0, 0)
+    else:
+        lax.fori_loop(0, count // step, group, 0)
+
+
 def encode(read, first, tiles, message):
     def widest(t, most):
         value = jnp.abs(read(first + t))
         return jnp.maximum(most, jnp.max(value.reshape(TILE // 8, 8, BLK), axis=0))
 
-    most = lax.fori_loop(0, tiles, widest, jnp.zeros((8, BLK), f32))
+    most = jnp.zeros((8, BLK), f32)
+    if tiles <= 12:
+        for t in range(tiles):
+            most = widest(t, most)
+    else:
+        most = lax.fori_loop(
+            0, tiles // 2, lambda t, m: widest(2 * t + 1, widest(2 * t, m)), most
+        )
     most = jnp.maximum(jnp.max(most, axis=0, keepdims=True) * 1.01, 1e-30)
     most = jnp.broadcast_to(most, (PAD, BLK)).astype(bf16)
     message[pl.ds(tiles * TILE, PAD), :] = most
     scale = SPAN / most.astype(f32)[:1]
 
-    def code(t, _):
+    def code(t):
         value = read(first + t)
         power = jnp.abs(value) * scale + LOW
         for _ in range(5):
             power = power * power
         message[tile(t), :] = jnp.where(value < 0, -power, power).astype(bf16)
-        return 0
-
-    lax.fori_loop(0, tiles, code, 0)
+
+    each(tiles, code)
 
 
 def decoder(message, tiles):
@@ -68,8 +96,10 @@
 
 def kernel(
     f_in, c_in, out, f_all, c_all, relay, ct, pt, s1, r1, s2, r2, zs, zr,
+    ws, wr, t1, u1, t2, u2,
     f_own, c_own, c_out, c_far_out, c_get, c_far, c_relay,
-    f_out, f_pass, f_relay, f_get, y1_out, y1_get, y2_out, y2_get, z_out, z_get,
+    f_out, f_pass, f_relay, f_get, f_far, y1_out, y1_get, y2_out, y2_get, z_out, z_get,
+    w_out, w_get, t1_out, t1_get, t2_out, t2_get,
 ):
     row, col = lax.axis_index("row"), lax.axis_index("col")
     y, z = lax.div(row, NZ), lax.rem(row, NZ)
@@ -174,8 +204,11 @@
         return pass_on(n, place(step, k), f_pass.at[n, slot], partner)
 
     def relayed(n):
-        d = 1 - 2 * lax.rem(n, 2)
-        return pass_on(n, place(-d, k), f_relay.at[n], on_x(d, k))
+        copies = []
+        for i, d in ways:
+            at = f_all.at[n, rows(place(-d, k) * TOK + i * HALF, HALF), :]
+            copies.append(send(at, at, f_relay.at[n, i], f_far.at[n, i], on_x(d, k)))
+        return copies
 
     def arrived(n, device):
         pass_on(n, device, f_out.at[n, 0], f_partner).wait_recv()
@@ -192,12 +225,14 @@
     def x1(n):
         arrived(n, place(1, k))
         arrived(n, place(-1, k))
-        relayed(n).start()
+        for copy in relayed(n):
+            copy.start()
         to_partner(n, 1, 0).start()
         to_partner(n, -1, 1).start()
 
     def x2(n):
-        arrived(n, place(2, k))
+        for copy in relayed(n):
+            copy.wait_recv()
         to_partner(n, 2, 2).start()
 
     x0(0)
@@ -205,10 +240,9 @@
         for c in (0, 1):
             far_first(way, d, c).wait_recv()
             far_second(way, d, c).start()
+    x1(0)
     x0(1)
     x0(2)
-    x1(0)
-    x2(0)
 
     keep.wait()
     for step, c in ((0, 1 - k), (1, 0), (1, 1), (-1, 0), (-1, 1)):
@@ -222,10 +256,11 @@
         ).wait_recv()
 
     def transpose(t, _):
-        ct[:, tile(t)] = c_all[tile(t), :].T
+        ct[:, wide(t)] = c_all[wide(t), :].T
         return 0
 
-    lax.fori_loop(0, GROUP // TILE, transpose, 0)
+    lax.fori_loop(0, GROUP // WIDE, transpose, 0)
+    x2(0)
 
     y_up, y_down = lax.rem(y + 1, NY), lax.rem(y + 3, NY)
     y_far = lax.rem(y + 2, NY)
@@ -270,16 +305,14 @@
             arriving[i].wait_recv()
             decode = decoder(r1.at[n, i], half)
 
-            def add(t, _):
+            def add(t):
                 at = tile(i * half + t)
                 pt[slot, target, at, :] += decode(t)
-                return 0
-
-            lax.fori_loop(0, half, add, 0)
-            encode(lambda t: pt[slot, target, tile(t), :], 0, COLS // TILE, s2.at[n, i])
+
+            each(half, add)
+            encode(lambda t: pt[slot, target, tile(t), :], 0, EARLY // TILE, s2.at[n, i])
             leaving[i].start()
 
-    whole = COLS + PAD
     part = H + PAD
 
     def z_half(i, d):
@@ -291,6 +324,98 @@
     def z_whole(n):
         d = 2 * lax.rem(n, 2) - 1
         return send(zs.at[n], zr.at[n], z_out.at[n], z_get.at[n], on_z(d))
+
+    def w_half(i, d, j):
+        return send(
+            ws.at[i * 7, j, pl.ds(0, L + PAD), :], wr.at[i * 7, j, pl.ds(0, L + PAD), :],
+            w_out.at[i * 7, j], w_get.at[i * 7, j], on_z(d),
+        )
+
+    def w_whole(n, j):
+        d = 2 * lax.rem(n, 2) - 1
+        return send(ws.at[n, j], wr.at[n, j], w_out.at[n, j], w_get.at[n, j], on_z(d))
+
+    def late_first(i, d):
+        return send(t1.at[i], u1.at[i], t1_out.at[i], t1_get.at[i], on_y(d))
+
+    def late_second(i, d):
+        return send(t2.at[i], u2.at[i], t2_out.at[i], t2_get.at[i], on_y(d))
+
+    base = EARLY // TILE
+
+    order = (y_far, y_up, y_down, y)
+
+    def late(n, which=range(NY)):
+        slot = lax.rem(n, 4)
+
+        def reader(yy):
+            return lambda t: pt[slot, yy, tile(base + t), :]
+
+        def join(slot_in, j, tiles, first):
+            decode = decoder(wr.at[slot_in, j], tiles)
+
+            def add(t):
+                pt[slot, order[j], tile(base + first + t), :] += decode(t)
+
+            each(tiles, add)
+
+        half, full = L // TILE, LATE // TILE
+
+        for j in which:
+
+            @pl.when(n == 0)
+            def _():
+                for i, d in ways:
+                    encode(reader(order[j]), i * half, half, ws.at[i * 7, j])
+                    w_half(i, d, j).start()
+
+            @pl.when(n == 1)
+            def _():
+                w_half(0, 1, j).wait_recv()
+                join(0, j, half, 0)
+
+            @pl.when(n == 2)
+            def _():
+                w_half(1, -1, j).wait_recv()
+                join(7, j, half, half)
+
+            @pl.when(n >= 3)
+            def _():
+                w_whole(n - 2, j).wait_recv()
+                join(n - 2, j, full, 0)
+
+            @pl.when((n >= 1) & (n < N - 1))
+            def _():
+                encode(reader(order[j]), 0, full, ws.at[n, j])
+                w_whole(n, j).start()
+
+            @pl.when(n == N - 1)
+            def _():
+                w_whole(n - 1, j).wait_recv()
+                join(n - 1, j, full, 0)
+                if j == 0:
+                    for i, d in ways:
+                        encode(reader(y_far), i * half, half, t1.at[i])
+                        late_first(i, d).start()
+
+    last = (N - 1) % 4
+
+    def late_middle():
+        for i, d in ways:
+            target = (y_up, y_down)[i]
+            late_first(i, d).wait_recv()
+            decode = decoder(u1.at[i], L // TILE)
+            for t in range(L // TILE):
+                pt[last, target, tile(base + i * (L // TILE) + t), :] += decode(t)
+            encode(lambda t: pt[last, target, tile(base + t), :], 0, LATE // TILE, t2.at[i])
+            late_second(i, d).start()
+
+    def late_end():
+        for i, d in ways:
+            late_second(i, d).wait_recv()
+            decode = decoder(u2.at[i], LATE // TILE)
+            for t in range(LATE // TILE):
+                pt[last, y, tile(base + t), :] += decode(t)
 
     def c(n):
         slot = lax.rem(n, 4)
@@ -298,14 +423,13 @@
         arriving = second_out(n)
         arriving[0].wait_recv()
         arriving[1].wait_recv()
-        up = decoder(r2.at[n, 0], COLS // TILE)
-        down = decoder(r2.at[n, 1], COLS // TILE)
-
-        def total(t, _):
+        up = decoder(r2.at[n, 0], EARLY // TILE)
+        down = decoder(r2.at[n, 1], EARLY // TILE)
+
+        def total(t):
             pt[slot, y, tile(t), :] += up(t) + down(t)
-            return 0
-
-        lax.fori_loop(0, COLS // TILE, total, 0)
+
+        each(EARLY // TILE, total)
 
         def read(t):
             return pt[slot, y, tile(t), :]
@@ -313,11 +437,10 @@
         def join(message, tiles, first):
             decode = decoder(message, tiles)
 
-            def add(t, _):
+            def add(t):
                 pt[slot, y, tile(first + t), :] += decode(t)
-                return 0
-
-            lax.fori_loop(0, tiles, add, 0)
+
+            each(tiles, add)
 
         @pl.when(n == 0)
         def _():
@@ -338,48 +461,60 @@
         @pl.when(n >= 3)
         def _():
             z_whole(n - 2).wait_recv()
-            join(zr.at[n - 2], COLS // TILE, 0)
+            join(zr.at[n - 2], EARLY // TILE, 0)
 
         @pl.when((n >= 1) & (n < N - 1))
         def _():
-            encode(read, 0, COLS // TILE, zs.at[n])
+            encode(read, 0, EARLY // TILE, zs.at[n])
             z_whole(n).start()
 
         @pl.when(n == N - 1)
         def _():
             z_whole(n - 1).wait_recv()
-            join(zr.at[n - 1], COLS // TILE, 0)
+            join(zr.at[n - 1], EARLY // TILE, 0)
+            late_end()
 
             def put(t, _):
-                out[:, tile(t)] = pt[slot, y, tile(t), :].T
+                out[:, wide(t)] = pt[slot, y, wide(t), :].T
                 return 0
 
-            lax.fori_loop(0, COLS // TILE, put, 0)
+            lax.fori_loop(0, COLS // WIDE, put, 0)
 
     def step(it, _):
         @pl.when(it < N)
         def _():
             a(it)
 
+        @pl.when(it == N - 1)
+        def _():
+            late(N - 1, (0,))
+
         @pl.when(it == 0)
         def _():
             x1(1)
-
-        @pl.when(it < N - 3)
-        def _():
-            x0(it + 3)
+            x0(3)
+
+        @pl.when((it >= 1) & (it < N + 1))
+        def _():
+            b(it - 1)
 
         @pl.when(it < N - 2)
         def _():
             x1(it + 2)
 
-        @pl.when((it >= 1) & (it < N + 1))
-        def _():
-            b(it - 1)
+        @pl.when(it < N - 4)
+        def _():
+            x0(it + 4)
 
         @pl.when(it < N - 1)
         def _():
             x2(it + 1)
+            late(it)
+
+        @pl.when(it == N)
+        def _():
+            late(N - 1, (1, 2, 3))
+            late_middle()
 
         @pl.when(it >= 2)
         def _():
@@ -394,21 +529,26 @@
             far_first(way, d, core).wait_send()
             far_second(way, d, core).wait_send()
         z_half(way, d).wait_send()
+        for j in range(NY):
+            w_half(way, d, j).wait_send()
+        late_first(way, d).wait_send()
+        late_second(way, d).wait_send()
     for copy in nears:
         copy.wait_send()
 
     def drain(n, _):
-        for copy in own_out(n) + first_out(n) + second_out(n):
+        for copy in own_out(n) + relayed(n) + first_out(n) + second_out(n):
             copy.wait_send()
         for i, hop in enumerate((1, -1, 2)):
             to_partner(n, hop, i).wait_send()
-        relayed(n).wait_send()
         return 0
 
     lax.fori_loop(0, N, drain, 0)
 
     def drain_z(n, _):
         z_whole(n).wait_send()
+        for j in range(NY):
+            w_whole(n, j).wait_send()
         return 0
 
     lax.fori_loop(1, N - 1, drain_z, 0)
@@ -418,7 +558,7 @@
     dma = pltpu.SemaphoreType.DMA
     return pl.pallas_call(
         kernel,
-        out_shape=jax.ShapeDtypeStruct((BLK, COLS), f32),
+        out_shape=pltpu.VMEM((BLK, COLS), f32),
         in_specs=[pl.BlockSpec(memory_space=pl.ANY)] * 2,
         out_specs=pl.BlockSpec(memory_space=pltpu.VMEM),
         scratch_shapes=[
@@ -429,13 +569,20 @@
             pltpu.VMEM((4, NY, COLS, BLK), f32),
             pltpu.VMEM((N, 2, H + PAD, BLK), bf16),
             pltpu.VMEM((N, 2, H + PAD, BLK), bf16),
-            pltpu.VMEM((N, 2, COLS + PAD, BLK), bf16),
-            pltpu.VMEM((N, 2, COLS + PAD, BLK), bf16),
-            pltpu.VMEM((N, COLS + PAD, BLK), bf16),
-            pltpu.VMEM((N, COLS + PAD, BLK), bf16),
+            pltpu.VMEM((N, 2, EARLY + PAD, BLK), bf16),
+            pltpu.VMEM((N, 2, EARLY + PAD, BLK), bf16),
+            pltpu.VMEM((N, EARLY + PAD, BLK), bf16),
+            pltpu.VMEM((N, EARLY + PAD, BLK), bf16),
+            pltpu.VMEM((N, NY, LATE + PAD, BLK), bf16),
+            pltpu.VMEM((N, NY, LATE + PAD, BLK), bf16),
+            pltpu.VMEM((2, L + PAD, BLK), bf16),
+            pltpu.VMEM((2, L + PAD, BLK), bf16),
+            pltpu.VMEM((2, LATE + PAD, BLK), bf16),
+            pltpu.VMEM((2, LATE + PAD, BLK), bf16),
             dma((N,)), dma((1,)), dma((5,)), dma((8,)), dma((8,)), dma((4,)), dma((4,)),
-            dma((N, 3)), dma((N, 3)), dma((N,)), dma((N, 8)),
+            dma((N, 3)), dma((N, 3)), dma((N, 2)), dma((N, 8)), dma((N, 2)),
             dma((N, 2)), dma((N, 2)), dma((N, 2)), dma((N, 2)), dma((N,)), dma((N,)),
+            dma((N, NY)), dma((N, NY)), dma((2,)), dma((2,)), dma((2,)), dma((2,)),
         ],
         compiler_params=pltpu.CompilerParams(
             collective_id=0, has_side_effects=True, vmem_limit_bytes=62 * 1024 * 1024

time: 151 us -> 124 us (0.82)
  Pallas kernels: 149 us -> 123 us
    pallas_call x1, Pallas kernels: 149 us -> 123 us  [local(): pl.pallas_call(kernel, out_shape=pltpu.VMEM((BLK, COLS), f32), in_specs=[...]
where the time goes in v2:
time: 124 us
  Pallas kernels  123 us (99%)
    pallas_call x1, Pallas kernels, local(): pl.pallas_call(kernel, out_shape=pltpu.VMEM((BLK, COLS), f32), in_specs=[...  123 us

profile of v2, /device:TPU:1, one launch (start us, length us, event | category | flops | bytes accessed | tf_op | source)
XLA Modules:
  0.0 124.2 jit_solution(15021677182742531693)
XLA Ops:
  0.0 123.4 %weight_grad.1 = f32[128,1024]{1,0:T(8,128)S(1)} custom-call(bf16[192,4096]{1,0:T(8,128)(2,1)} %f_in.1, bf16[192,8192]{1,0:T(8,128)(2,1)} %c_in.1), custom_call_target="tpu_custom_call" | custom-call | tf_op jit(solution)/shard_map/weight_grad/pallas_call | solution.py:559
  123.4 0.8 copy.4

commit v3 on v2

--- a/solution.py
+++ b/solution.py
@@ -15,7 +15,7 @@
 N = NZ
 TILE = 32
 WIDE = 128
-LATE = 320
+LATE = 384
 EARLY = COLS - LATE
 H = EARLY // 2
 L = LATE // 2
@@ -97,9 +97,9 @@
 def kernel(
     f_in, c_in, out, f_all, c_all, relay, ct, pt, s1, r1, s2, r2, zs, zr,
     ws, wr, t1, u1, t2, u2,
-    f_own, c_own, c_out, c_far_out, c_get, c_far, c_relay,
-    f_out, f_pass, f_relay, f_get, f_far, y1_out, y1_get, y2_out, y2_get, z_out, z_get,
-    w_out, w_get, t1_out, t1_get, t2_out, t2_get,
+    f_own, c_own, c_out, c_relay, c_get, f_send, f_near, f_far, f_mate,
+    y1_out, y1_get, y2_out, y2_get, z_out, z_get, w_out, w_get,
+    t1_out, t1_get, t2_out, t2_get,
 ):
     row, col = lax.axis_index("row"), lax.axis_index("col")
     y, z = lax.div(row, NZ), lax.rem(row, NZ)
@@ -125,16 +125,25 @@
 
     partner = on_x(0, 1 - k)
 
+    def left(ref, sem):
+        send(ref, ref, sem, c_get.at[0], partner).wait_send()
+
+    def landed(ref, sem):
+        send(ref, ref, c_out.at[0], sem, partner).wait_recv()
+
+    FAR, UP, DOWN, OWN = range(NY)
+    order = (lax.rem(y + 2, NY), lax.rem(y + 1, NY), lax.rem(y + 3, NY), y)
+
     def offset(n):
         far = N // 2 - lax.div(n + 1, 2)
         return lax.rem(z + far * (2 * lax.rem(n, 2) - 1) + NZ, NZ)
 
     def own_features(n, _):
-        for yy in range(NY):
-            at = pl.multiple_of((yy * NZ + offset(n)) * BLK, BLK)
+        for j in range(NY):
+            at = pl.multiple_of((order[j] * NZ + offset(n)) * BLK, BLK)
             pltpu.make_async_copy(
                 f_in.at[:, pl.ds(at, BLK)],
-                f_all.at[n, rows(col * TOK, TOK), pl.ds(yy * BLK, BLK)],
+                f_all.at[n, rows(col * TOK, TOK), pl.ds(j * BLK, BLK)],
                 f_own.at[n],
             ).start()
         return 0
@@ -162,25 +171,24 @@
     def far_first(way, d, c):
         return send(
             c_in.at[pl.ds(way * HALF, HALF), columns(place(2, c))],
-            relay.at[way * 2 + c], c_far_out.at[way * 2 + c], c_relay.at[way * 2 + c],
+            relay.at[way * 2 + c], c_out.at[1], c_relay.at[way * 2 + c],
             on_x(d, k),
         )
 
     def far_second(way, d, c):
         at = rows(place(-d, k) * TOK + way * HALF, HALF)
         return send(
-            relay.at[way * 2 + c], c_all.at[at, :],
-            c_far_out.at[4 + way * 2 + c], c_far.at[way * 2 + k], on_x(d, c),
-        )
-
-    def near(step, c, slot):
+            relay.at[way * 2 + c], c_all.at[at, :], c_out.at[1], c_get.at[0], on_x(d, c),
+        )
+
+    def near(step, c):
         return send(
             c_in.at[:, columns(place(step, c))], c_all.at[rows(col * TOK, TOK), :],
-            c_out.at[slot], c_get.at[col], on_x(step, c),
-        )
-
-    nears = [near(d, c, way * 2 + c) for way, d in ways for c in (0, 1)]
-    nears.append(near(0, 1 - k, 4))
+            c_out.at[0], c_get.at[0], on_x(step, c),
+        )
+
+    nears = [near(d, c) for _, d in ways for c in (0, 1)]
+    nears.append(near(0, 1 - k))
     for way, d in ways:
         for c in (0, 1):
             far_first(way, d, c).start()
@@ -190,30 +198,28 @@
     def block(n, device):
         return f_all.at[n, rows(device * TOK, TOK), :]
 
-    def pass_on(n, device, out_sem, to):
-        return send(block(n, device), block(n, device), out_sem, f_get.at[n, device], to)
+    def pass_on(n, device, out_sem, get_sem, to):
+        return send(block(n, device), block(n, device), out_sem, get_sem, to)
 
     def own_out(n):
         return [
-            pass_on(n, col, f_out.at[n, 0], on_x(1, k)),
-            pass_on(n, col, f_out.at[n, 1], on_x(-1, k)),
-            pass_on(n, col, f_out.at[n, 2], partner),
+            pass_on(n, col, f_send.at[0], f_near.at[n], on_x(1, k)),
+            pass_on(n, col, f_send.at[0], f_near.at[n], on_x(-1, k)),
+            pass_on(n, col, f_send.at[0], f_mate.at[n], partner),
         ]
 
-    def to_partner(n, step, slot):
-        return pass_on(n, place(step, k), f_pass.at[n, slot], partner)
+    def to_partner(n, step):
+        return pass_on(n, place(step, k), f_send.at[1], f_mate.at[n], partner)
 
     def relayed(n):
         copies = []
         for i, d in ways:
             at = f_all.at[n, rows(place(-d, k) * TOK + i * HALF, HALF), :]
-            copies.append(send(at, at, f_relay.at[n, i], f_far.at[n, i], on_x(d, k)))
+            copies.append(send(at, at, f_send.at[2], f_far.at[n], on_x(d, k)))
         return copies
 
-    def arrived(n, device):
-        pass_on(n, device, f_out.at[n, 0], f_partner).wait_recv()
-
-    f_partner = partner
+    def blocks(n, count):
+        return f_all.at[n, pl.ds(0, count * TOK), :]
 
     def x0(n):
         pltpu.make_async_copy(
@@ -223,17 +229,15 @@
             copy.start()
 
     def x1(n):
-        arrived(n, place(1, k))
-        arrived(n, place(-1, k))
+        landed(blocks(n, 2), f_near.at[n])
         for copy in relayed(n):
             copy.start()
-        to_partner(n, 1, 0).start()
-        to_partner(n, -1, 1).start()
+        to_partner(n, 1).start()
+        to_partner(n, -1).start()
 
     def x2(n):
-        for copy in relayed(n):
-            copy.wait_recv()
-        to_partner(n, 2, 2).start()
+        landed(blocks(n, 1), f_far.at[n])
+        to_partner(n, 2).start()
 
     x0(0)
     for way, d in ways:
@@ -245,15 +249,7 @@
     x0(2)
 
     keep.wait()
-    for step, c in ((0, 1 - k), (1, 0), (1, 1), (-1, 0), (-1, 1)):
-        send(
-            c_in.at[:, columns(0)], c_all.at[rows(0, TOK), :],
-            c_out.at[0], c_get.at[place(step, c)], partner,
-        ).wait_recv()
-    for i in range(4):
-        send(
-            relay.at[i], c_all.at[rows(0, HALF), :], c_out.at[0], c_far.at[i], partner
-        ).wait_recv()
+    landed(c_all.at[pl.ds(0, 7 * TOK), :], c_get.at[0])
 
     def transpose(t, _):
         ct[:, wide(t)] = c_all[wide(t), :].T
@@ -262,37 +258,28 @@
     lax.fori_loop(0, GROUP // WIDE, transpose, 0)
     x2(0)
 
-    y_up, y_down = lax.rem(y + 1, NY), lax.rem(y + 3, NY)
-    y_far = lax.rem(y + 2, NY)
-
     def first_out(n):
         return [
-            send(s1.at[n, i], r1.at[n, i], y1_out.at[n, i], y1_get.at[n, i], on_y(d))
+            send(s1.at[n, i], r1.at[n, i], y1_out.at[0], y1_get.at[n, i], on_y(d))
             for i, d in ways
         ]
 
     def second_out(n):
         return [
-            send(s2.at[n, i], r2.at[n, i], y2_out.at[n, i], y2_get.at[n, i], on_y(d))
+            send(s2.at[n, i], r2.at[n, i], y2_out.at[0], y2_get.at[n], on_y(d))
             for i, d in ways
         ]
 
     def a(n):
         slot = lax.rem(n, 4)
-        for c in range(NX):
-            arrived(n, c * 2 + 1 - k)
-
-        def product(m, _):
-            at = pl.ds(pl.multiple_of(m * 256, 256), 256)
-            value = jnp.dot(ct[at, :], f_all[n], preferred_element_type=f32)
-            for yy in range(NY):
-                pt[slot, yy, at, :] = value[:, yy * BLK : (yy + 1) * BLK]
-            return 0
-
-        lax.fori_loop(0, COLS // 256, product, 0)
+        landed(blocks(n, 4), f_mate.at[n])
+
+        value = jnp.dot(ct[...], f_all[n], preferred_element_type=f32)
+        for j in range(NY):
+            pt[slot, j] = value[:, j * BLK : (j + 1) * BLK]
         half = H // TILE
         for i in (0, 1):
-            encode(lambda t: pt[slot, y_far, tile(t), :], i * half, half, s1.at[n, i])
+            encode(lambda t: pt[slot, FAR, tile(t), :], i * half, half, s1.at[n, i])
         for copy in first_out(n):
             copy.start()
 
@@ -301,7 +288,7 @@
         half = H // TILE
         arriving = first_out(n)
         leaving = second_out(n)
-        for i, target in ((0, y_up), (1, y_down)):
+        for i, target in ((0, UP), (1, DOWN)):
             arriving[i].wait_recv()
             decode = decoder(r1.at[n, i], half)
 
@@ -318,44 +305,42 @@
     def z_half(i, d):
         return send(
             zs.at[i * 7, pl.ds(0, part), :], zr.at[i * 7, pl.ds(0, part), :],
-            z_out.at[i * 7], z_get.at[i * 7], on_z(d),
+            z_out.at[1], z_get.at[i * 7], on_z(d),
         )
 
     def z_whole(n):
         d = 2 * lax.rem(n, 2) - 1
-        return send(zs.at[n], zr.at[n], z_out.at[n], z_get.at[n], on_z(d))
+        return send(zs.at[n], zr.at[n], z_out.at[0], z_get.at[n], on_z(d))
 
     def w_half(i, d, j):
         return send(
             ws.at[i * 7, j, pl.ds(0, L + PAD), :], wr.at[i * 7, j, pl.ds(0, L + PAD), :],
-            w_out.at[i * 7, j], w_get.at[i * 7, j], on_z(d),
+            w_out.at[1], w_get.at[i * 7, j], on_z(d),
         )
 
     def w_whole(n, j):
         d = 2 * lax.rem(n, 2) - 1
-        return send(ws.at[n, j], wr.at[n, j], w_out.at[n, j], w_get.at[n, j], on_z(d))
+        return send(ws.at[n, j], wr.at[n, j], w_out.at[0], w_get.at[n, j], on_z(d))
 
     def late_first(i, d):
-        return send(t1.at[i], u1.at[i], t1_out.at[i], t1_get.at[i], on_y(d))
+        return send(t1.at[i], u1.at[i], t1_out.at[0], t1_get.at[i], on_y(d))
 
     def late_second(i, d):
-        return send(t2.at[i], u2.at[i], t2_out.at[i], t2_get.at[i], on_y(d))
+        return send(t2.at[i], u2.at[i], t2_out.at[0], t2_get.at[i], on_y(d))
 
     base = EARLY // TILE
-
-    order = (y_far, y_up, y_down, y)
 
     def late(n, which=range(NY)):
         slot = lax.rem(n, 4)
 
-        def reader(yy):
-            return lambda t: pt[slot, yy, tile(base + t), :]
+        def reader(j):
+            return lambda t: pt[slot, j, tile(base + t), :]
 
         def join(slot_in, j, tiles, first):
             decode = decoder(wr.at[slot_in, j], tiles)
 
             def add(t):
-                pt[slot, order[j], tile(base + first + t), :] += decode(t)
+                pt[slot, j, tile(base + first + t), :] += decode(t)
 
             each(tiles, add)
 
@@ -366,7 +351,7 @@
             @pl.when(n == 0)
             def _():
                 for i, d in ways:
-                    encode(reader(order[j]), i * half, half, ws.at[i * 7, j])
+                    encode(reader(j), i * half, half, ws.at[i * 7, j])
                     w_half(i, d, j).start()
 
             @pl.when(n == 1)
@@ -386,7 +371,7 @@
 
             @pl.when((n >= 1) & (n < N - 1))
             def _():
-                encode(reader(order[j]), 0, full, ws.at[n, j])
+                encode(reader(j), 0, full, ws.at[n, j])
                 w_whole(n, j).start()
 
             @pl.when(n == N - 1)
@@ -395,14 +380,14 @@
                 join(n - 1, j, full, 0)
                 if j == 0:
                     for i, d in ways:
-                        encode(reader(y_far), i * half, half, t1.at[i])
+                        encode(reader(FAR), i * half, half, t1.at[i])
                         late_first(i, d).start()
 
     last = (N - 1) % 4
 
     def late_middle():
         for i, d in ways:
-            target = (y_up, y_down)[i]
+            target = (UP, DOWN)[i]
             late_first(i, d).wait_recv()
             decode = decoder(u1.at[i], L // TILE)
             for t in range(L // TILE):
@@ -415,30 +400,28 @@
             late_second(i, d).wait_recv()
             decode = decoder(u2.at[i], LATE // TILE)
             for t in range(LATE // TILE):
-                pt[last, y, tile(base + t), :] += decode(t)
+                pt[last, OWN, tile(base + t), :] += decode(t)
 
     def c(n):
         slot = lax.rem(n, 4)
         half = H // TILE
-        arriving = second_out(n)
-        arriving[0].wait_recv()
-        arriving[1].wait_recv()
+        landed(r2.at[n], y2_get.at[n])
         up = decoder(r2.at[n, 0], EARLY // TILE)
         down = decoder(r2.at[n, 1], EARLY // TILE)
 
         def total(t):
-            pt[slot, y, tile(t), :] += up(t) + down(t)
+            pt[slot, OWN, tile(t), :] += up(t) + down(t)
 
         each(EARLY // TILE, total)
 
         def read(t):
-            return pt[slot, y, tile(t), :]
+            return pt[slot, OWN, tile(t), :]
 
         def join(message, tiles, first):
             decode = decoder(message, tiles)
 
             def add(t):
-                pt[slot, y, tile(first + t), :] += decode(t)
+                pt[slot, OWN, tile(first + t), :] += decode(t)
 
             each(tiles, add)
 
@@ -475,7 +458,7 @@
             late_end()
 
             def put(t, _):
-                out[:, wide(t)] = pt[slot, y, wide(t), :].T
+                out[:, wide(t)] = pt[slot, OWN, wide(t), :].T
                 return 0
 
             lax.fori_loop(0, COLS // WIDE, put, 0)
@@ -494,7 +477,7 @@
             x1(1)
             x0(3)
 
-        @pl.when((it >= 1) & (it < N + 1))
+        @pl.when((it >= 2) & (it < N + 1))
         def _():
             b(it - 1)
 
@@ -505,18 +488,27 @@
         @pl.when(it < N - 4)
         def _():
             x0(it + 4)
+
+        @pl.when((it >= 3) & (it < N))
+        def _():
+            c(it - 3)
 
         @pl.when(it < N - 1)
         def _():
             x2(it + 1)
             late(it)
 
+        @pl.when(it == 0)
+        def _():
+            b(0)
+
         @pl.when(it == N)
         def _():
             late(N - 1, (1, 2, 3))
             late_middle()
-
-        @pl.when(it >= 2)
+            c(N - 3)
+
+        @pl.when(it >= N)
         def _():
             c(it - 2)
 
@@ -524,34 +516,19 @@
 
     lax.fori_loop(0, N + 2, step, 0)
 
-    for way, d in ways:
-        for core in (0, 1):
-            far_first(way, d, core).wait_send()
-            far_second(way, d, core).wait_send()
-        z_half(way, d).wait_send()
-        for j in range(NY):
-            w_half(way, d, j).wait_send()
-        late_first(way, d).wait_send()
-        late_second(way, d).wait_send()
-    for copy in nears:
-        copy.wait_send()
-
-    def drain(n, _):
-        for copy in own_out(n) + relayed(n) + first_out(n) + second_out(n):
-            copy.wait_send()
-        for i, hop in enumerate((1, -1, 2)):
-            to_partner(n, hop, i).wait_send()
-        return 0
-
-    lax.fori_loop(0, N, drain, 0)
-
-    def drain_z(n, _):
-        z_whole(n).wait_send()
-        for j in range(NY):
-            w_whole(n, j).wait_send()
-        return 0
-
-    lax.fori_loop(1, N - 1, drain_z, 0)
+    left(c_all.at[pl.ds(0, 5 * TOK), :], c_out.at[0])
+    left(c_all.at[pl.ds(0, 4 * TOK), :], c_out.at[1])
+    left(f_all.at[pl.ds(0, 3)], f_send.at[0])
+    left(f_all.at[pl.ds(0, 3)], f_send.at[1])
+    left(f_all.at[0], f_send.at[2])
+    left(s1, y1_out.at[0])
+    left(s2, y2_out.at[0])
+    left(zs.at[pl.ds(1, N - 2)], z_out.at[0])
+    left(s1.at[0], z_out.at[1])
+    left(ws.at[pl.ds(1, N - 2)], w_out.at[0])
+    left(ws.at[pl.ds(0, 2), :, pl.ds(0, L + PAD), :], w_out.at[1])
+    left(t1, t1_out.at[0])
+    left(t2, t2_out.at[0])
 
 
 def local(features, cotangent):
@@ -579,10 +556,9 @@
             pltpu.VMEM((2, L + PAD, BLK), bf16),
             pltpu.VMEM((2, LATE + PAD, BLK), bf16),
             pltpu.VMEM((2, LATE + PAD, BLK), bf16),
-            dma((N,)), dma((1,)), dma((5,)), dma((8,)), dma((8,)), dma((4,)), dma((4,)),
-            dma((N, 3)), dma((N, 3)), dma((N, 2)), dma((N, 8)), dma((N, 2)),
-            dma((N, 2)), dma((N, 2)), dma((N, 2)), dma((N, 2)), dma((N,)), dma((N,)),
-            dma((N, NY)), dma((N, NY)), dma((2,)), dma((2,)), dma((2,)), dma((2,)),
+            dma((N,)), dma((1,)), dma((2,)), dma((4,)), dma((1,)), dma((3,)), dma((N,)),
+            dma((N,)), dma((N,)), dma((1,)), dma((N, 2)), dma((1,)), dma((N,)), dma((2,)),
+            dma((N,)), dma((2,)), dma((N, NY)), dma((1,)), dma((2,)), dma((1,)), dma((2,)),
         ],
         compiler_params=pltpu.CompilerParams(
             collective_id=0, has_side_effects=True, vmem_limit_bytes=62 * 1024 * 1024

time: 124 us -> 121 us (0.976)
  Pallas kernels: 123 us -> 120 us
    pallas_call x1, Pallas kernels: 123 us -> 120 us  [local(): pl.pallas_call(kernel, out_shape=pltpu.VMEM((BLK, COLS), f32), in_specs=[...]
where the time goes in v3:
time: 121 us
  Pallas kernels  120 us (99%)
    pallas_call x1, Pallas kernels, local(): pl.pallas_call(kernel, out_shape=pltpu.VMEM((BLK, COLS), f32), in_specs=[...  120 us

profile of v3, /device:TPU:1, one launch (start us, length us, event | category | flops | bytes accessed | tf_op | source)
XLA Modules:
  0.0 120.6 jit_solution(12134714097881407776)
XLA Ops:
  0.0 119.8 %weight_grad.1 = f32[128,1024]{1,0:T(8,128)S(1)} custom-call(bf16[192,4096]{1,0:T(8,128)(2,1)} %f_in.1, bf16[192,8192]{1,0:T(8,128)(2,1)} %c_in.1), custom_call_target="tpu_custom_call" | custom-call | tf_op jit(solution)/shard_map/weight_grad/pallas_call | solution.py:536
  119.8 0.8 copy.4

commit v4 on v3

--- a/solution.py
+++ b/solution.py
@@ -168,32 +168,51 @@
 
     ways = ((0, 1), (1, -1))
 
-    def far_first(way, d, c):
+    cuts = ((0, EARLY), (EARLY, LATE))
+
+    def piece(device, p):
+        start, size = cuts[p]
+        return pl.ds(pl.multiple_of(device * COLS + start, WIDE), size)
+
+    def cut(p):
+        return pl.ds(cuts[p][0], cuts[p][1])
+
+    def far_first(p, way, d, c):
+        i = way * 2 + c
         return send(
-            c_in.at[pl.ds(way * HALF, HALF), columns(place(2, c))],
-            relay.at[way * 2 + c], c_out.at[1], c_relay.at[way * 2 + c],
-            on_x(d, k),
-        )
-
-    def far_second(way, d, c):
+            c_in.at[pl.ds(way * HALF, HALF), piece(place(2, c), p)],
+            relay.at[i, :, cut(p)], c_out.at[1], c_relay.at[p, i], on_x(d, k),
+        )
+
+    def far_second(p, way, d, c):
         at = rows(place(-d, k) * TOK + way * HALF, HALF)
         return send(
-            relay.at[way * 2 + c], c_all.at[at, :], c_out.at[1], c_get.at[0], on_x(d, c),
-        )
-
-    def near(step, c):
+            relay.at[way * 2 + c, :, cut(p)], c_all.at[at, cut(p)],
+            c_out.at[1], c_get.at[p], on_x(d, c),
+        )
+
+    def near(p, step, c):
         return send(
-            c_in.at[:, columns(place(step, c))], c_all.at[rows(col * TOK, TOK), :],
-            c_out.at[0], c_get.at[0], on_x(step, c),
-        )
-
-    nears = [near(d, c) for _, d in ways for c in (0, 1)]
-    nears.append(near(0, 1 - k))
-    for way, d in ways:
-        for c in (0, 1):
-            far_first(way, d, c).start()
-    for copy in nears:
-        copy.start()
+            c_in.at[:, piece(place(step, c), p)], c_all.at[rows(col * TOK, TOK), cut(p)],
+            c_out.at[0], c_get.at[p], on_x(step, c),
+        )
+
+    def far_start(p):
+        for way, d in ways:
+            for c in (0, 1):
+                far_first(p, way, d, c).start()
+
+    def near_start(p):
+        for _, d in ways:
+            for c in (0, 1):
+                near(p, d, c).start()
+        near(p, 0, 1 - k).start()
+
+    def far_on(p):
+        for way, d in ways:
+            for c in (0, 1):
+                far_first(p, way, d, c).wait_recv()
+                far_second(p, way, d, c).start()
 
     def block(n, device):
         return f_all.at[n, rows(device * TOK, TOK), :]
@@ -239,24 +258,30 @@
         landed(blocks(n, 1), f_far.at[n])
         to_partner(n, 2).start()
 
+    def transpose(p):
+        landed(c_all.at[pl.ds(0, 7 * TOK), cut(p)], c_get.at[p])
+
+        def one(t, _):
+            ct[cut(p), wide(t)] = c_all[wide(t), cut(p)].T
+            return 0
+
+        lax.fori_loop(0, GROUP // WIDE, one, 0)
+
+    far_start(0)
+    near_start(0)
     x0(0)
-    for way, d in ways:
-        for c in (0, 1):
-            far_first(way, d, c).wait_recv()
-            far_second(way, d, c).start()
+    far_on(0)
+    x0(1)
     x1(0)
-    x0(1)
+    far_start(1)
+    x1(1)
+    near_start(1)
+    keep.wait()
+    transpose(0)
+    x2(0)
+    far_on(1)
     x0(2)
-
-    keep.wait()
-    landed(c_all.at[pl.ds(0, 7 * TOK), :], c_get.at[0])
-
-    def transpose(t, _):
-        ct[:, wide(t)] = c_all[wide(t), :].T
-        return 0
-
-    lax.fori_loop(0, GROUP // WIDE, transpose, 0)
-    x2(0)
+    x0(3)
 
     def first_out(n):
         return [
@@ -270,18 +295,29 @@
             for i, d in ways
         ]
 
-    def a(n):
-        slot = lax.rem(n, 4)
-        landed(blocks(n, 4), f_mate.at[n])
-
-        value = jnp.dot(ct[...], f_all[n], preferred_element_type=f32)
+    def product(n, at):
+        value = jnp.dot(ct[at, :], f_all[n], preferred_element_type=f32)
         for j in range(NY):
-            pt[slot, j] = value[:, j * BLK : (j + 1) * BLK]
+            pt[lax.rem(n, 4), j, at, :] = value[:, j * BLK : (j + 1) * BLK]
+
+    def first(n):
         half = H // TILE
         for i in (0, 1):
-            encode(lambda t: pt[slot, FAR, tile(t), :], i * half, half, s1.at[n, i])
+            read = lambda t: pt[lax.rem(n, 4), FAR, tile(t), :]
+            encode(read, i * half, half, s1.at[n, i])
         for copy in first_out(n):
             copy.start()
+
+    def a(n):
+        @pl.when(n >= 2)
+        def _():
+            landed(blocks(n, 4), f_mate.at[n])
+            product(n, pl.ds(0, COLS))
+            first(n)
+
+        @pl.when(n < 2)
+        def _():
+            product(n, cut(1))
 
     def b(n):
         slot = lax.rem(n, 4)
@@ -382,6 +418,11 @@
                     for i, d in ways:
                         encode(reader(FAR), i * half, half, t1.at[i])
                         late_first(i, d).start()
+
+    def ahead(n):
+        landed(blocks(n, 4), f_mate.at[n])
+        product(n, cut(0))
+        first(n)
 
     last = (N - 1) % 4
 
@@ -468,15 +509,14 @@
         def _():
             a(it)
 
+        @pl.when(it == N - 2)
+        def _():
+            late(N - 3)
+
         @pl.when(it == N - 1)
         def _():
             late(N - 1, (0,))
 
-        @pl.when(it == 0)
-        def _():
-            x1(1)
-            x0(3)
-
         @pl.when((it >= 2) & (it < N + 1))
         def _():
             b(it - 1)
@@ -493,14 +533,13 @@
         def _():
             c(it - 3)
 
-        @pl.when(it < N - 1)
+        @pl.when((it >= 1) & (it < N - 1))
         def _():
             x2(it + 1)
+
+        @pl.when((it < N - 1) & (it != N - 3))
+        def _():
             late(it)
-
-        @pl.when(it == 0)
-        def _():
-            b(0)
 
         @pl.when(it == N)
         def _():
@@ -514,6 +553,11 @@
 
         return 0
 
+    ahead(0)
+    x2(1)
+    ahead(1)
+    b(0)
+    transpose(1)
     lax.fori_loop(0, N + 2, step, 0)
 
     left(c_all.at[pl.ds(0, 5 * TOK), :], c_out.at[0])
@@ -556,7 +600,7 @@
             pltpu.VMEM((2, L + PAD, BLK), bf16),
             pltpu.VMEM((2, LATE + PAD, BLK), bf16),
             pltpu.VMEM((2, LATE + PAD, BLK), bf16),
-            dma((N,)), dma((1,)), dma((2,)), dma((4,)), dma((1,)), dma((3,)), dma((N,)),
+            dma((N,)), dma((1,)), dma((2,)), dma((2, 4)), dma((2,)), dma((3,)), dma((N,)),
             dma((N,)), dma((N,)), dma((1,)), dma((N, 2)), dma((1,)), dma((N,)), dma((2,)),
             dma((N,)), dma((2,)), dma((N, NY)), dma((1,)), dma((2,)), dma((1,)), dma((2,)),
         ],

time: 121 us -> 121 us (level)
  no operation moved by 1% of the time
where the time goes in v4:
time: 121 us
  Pallas kernels  120 us (99%)
    pallas_call x1, Pallas kernels, local(): pl.pallas_call(kernel, out_shape=pltpu.VMEM((BLK, COLS), f32), in_specs=[...  120 us

profile of v4, /device:TPU:1, one launch (start us, length us, event | category | flops | bytes accessed | tf_op | source)
XLA Modules:
  0.0 120.9 jit_solution(2372011995488422257)
XLA Ops:
  0.0 120.1 %weight_grad.1 = f32[128,1024]{1,0:T(8,128)S(1)} custom-call(bf16[192,4096]{1,0:T(8,128)(2,1)} %f_in.1, bf16[192,8192]{1,0:T(8,128)(2,1)} %c_in.1), custom_call_target="tpu_custom_call" | custom-call | tf_op jit(solution)/shard_map/weight_grad/pallas_call | solution.py:580
  120.2 0.8 copy.4
